TPU v7x, 32 devices: a whole 2x2x4 slice. The times are simulated.
32 devices in a mesh: dp: 8 (over z, x), fsdp: 4 (over y, core).
Axes of the slice: x: 2, y: 2, z: 4, core: 2. Of those that a mesh axis runs over, the one named last changes fastest.
Arguments:
- hidden: bfloat16 [16, 256, 5120], P('dp', None, 'fsdp'), may hold values from -8 to 8
- gain: bfloat16 [5120], P('fsdp'), may hold values from 0.25 to 1.75
- head: bfloat16 [2048, 5120], P('fsdp'), may hold values from -1 to 1
- targets: int32 [16, 256], P('dp'), may hold values from 0 to 2047, as said below
- lengths: int32 [16], P('dp'), may hold values from 1 to 256, 2048 in all
- old_logp: float32 [16, 256], P('dp'), may hold values from -64 to 0
- rewards: float32 [16], P('dp'), may hold values from -6 to 6
- group_slot: int32 [16], P('dp'), may hold values from 0 to 15, each once
Outputs:
- loss: float32 [], replicated
- grad_hidden: bfloat16 [16, 256, 5120], P('dp', None, 'fsdp')
- grad_gain: float32 [5120], P('fsdp')
- grad_head_t: float32 [5120, 2048], P('dp', 'fsdp')
Inputs may be any that keep to these rules, and one draw needn't show every extreme that they name: `lengths`: they sum to 2048 and one of them equals 256. `group_slot`: each value once; responses with equal group_slot // 8 answer one prompt. At position 0, different responses have different targets.
All inputs are finite; a program needn't handle non-finite values. No bound on the sum of `lengths` on one device may be relied on, other than what follows from the above.
Results may differ from a plain program's by a relative error of at most 0.018.
Values may be sent and summed in bfloat16 or wider, within the bound.
A program may use at most 64 MiB of HBM per device.

v0:
```python
import jax
import jax.numpy as jnp
from jax import lax
from jax.sharding import PartitionSpec as P

GROUP = 8


eps_norm = 1e-06
clip_low = 0.8
clip_high = 1.2
dual_bound = 3.0


def body(hidden, gain, head, targets, lengths, old_logp, rewards, group_slot):
    resp_here, length_max, shard_cols = hidden.shape
    rows = resp_here * length_max
    whole, gain_full = (
        lax.all_gather(hidden, "fsdp", axis=2, tiled=True),
        lax.all_gather(gain, "fsdp", axis=0, tiled=True),
    )
    width = whole.shape[2]
    whole = whole.reshape(rows, width)
    vocab_here = head.shape[0]
    vocab_start = lax.axis_index("fsdp") * vocab_here
    groups_all = resp_here * lax.axis_size("dp") // GROUP
    group = group_slot // GROUP
    member = (group[:, None] == jnp.arange(groups_all, dtype=jnp.int32)[None, :]).astype(
        jnp.float32
    )
    local_sums = jnp.sum(member * rewards[:, None], axis=0)
    local_count = jnp.sum(lengths).astype(jnp.float32)
    group_sums, count = lax.psum((local_sums, local_count), "dp")
    adv_resp = rewards - jnp.sum(member * group_sums[None, :], axis=1) / GROUP
    adv = jnp.repeat(adv_resp, length_max)
    mask = (
        (jnp.arange(length_max, dtype=jnp.int32)[None, :] < lengths[:, None])
        .astype(jnp.float32)
        .reshape(rows)
    )
    gain_f = gain_full.astype(jnp.float32)
    inv = lax.rsqrt(
        jnp.mean(jnp.square(whole.astype(jnp.float32)), axis=1, keepdims=True) + eps_norm
    )
    normed = (whole.astype(jnp.float32) * inv * gain_f).astype(jnp.bfloat16)
    logits = lax.dot_general(
        normed, head, (((1,), (1,)), ((), ())), preferred_element_type=jnp.float32
    )
    top_local = jnp.max(logits, axis=1)
    sum_local = jnp.sum(jnp.exp(logits - top_local[:, None]), axis=1)
    local_targets = targets.reshape(rows) - vocab_start
    hits = jnp.arange(vocab_here, dtype=jnp.int32)[None, :] == local_targets[:, None]
    chosen_local = jnp.sum(jnp.where(hits, logits, 0.0), axis=1)
    top = lax.pmax(top_local, "fsdp")
    total, chosen = lax.psum((sum_local * jnp.exp(top_local - top), chosen_local), "fsdp")
    lse = top + jnp.log(total)
    logp = chosen - lse
    ratio = jnp.exp(logp - old_logp.reshape(rows))
    first = ratio * adv
    second = jnp.clip(ratio, clip_low, clip_high) * adv
    policy = -jnp.minimum(first, second)
    policy = jnp.where(adv < 0, jnp.minimum(policy, -dual_bound * adv), policy)
    loss_local = jnp.sum(mask * policy)
    active = (first <= second) & jnp.logical_not((adv < 0) & (first < dual_bound * adv))
    slots_all = rows * lax.axis_size("dp")
    grad_logp = slots_all / count * mask * jnp.where(active, -ratio * adv, 0.0)
    probs = jnp.exp(logits - lse[:, None])
    dlogits = (grad_logp[:, None] * (hits.astype(jnp.float32) - probs)).astype(jnp.bfloat16)
    dn_part = jnp.dot(dlogits, head, preferred_element_type=jnp.float32)
    h_share = hidden.reshape(rows, shard_cols).astype(jnp.float32)
    gain_share = gain.astype(jnp.float32)
    dn_share = lax.psum_scatter(
        dn_part.astype(jnp.bfloat16), "fsdp", scatter_dimension=1, tiled=True
    ).astype(jnp.float32)
    dots = lax.psum(jnp.sum(h_share * (dn_share * gain_share), axis=1), "fsdp")
    dy = dn_share * gain_share
    grad_h = inv * dy - h_share * inv * inv * inv * dots[:, None] / width
    gain_part = jnp.sum(dn_share * h_share * inv, axis=0)
    grad_head_t = lax.psum_scatter(
        lax.dot_general(
            normed, dlogits, (((0,), (0,)), ((), ())), preferred_element_type=jnp.float32
        ).astype(jnp.bfloat16),
        "dp",
        scatter_dimension=0,
        tiled=True,
    ).astype(jnp.float32)
    loss_sum, grad_gain = lax.psum((loss_local, gain_part), "dp")
    loss = loss_sum / count
    grad_hidden = grad_h.astype(jnp.bfloat16).reshape(resp_here, length_max, shard_cols)
    return (loss, grad_hidden, grad_gain, grad_head_t)


def solution(mesh):
    in_specs = (
        P("dp", None, "fsdp"),
        P("fsdp"),
        P("fsdp", None),
        P("dp", None),
        P("dp"),
        P("dp", None),
        P("dp"),
        P("dp"),
    )
    out_specs = (P(), P("dp", None, "fsdp"), P("fsdp"), P("dp", "fsdp"))
    return jax.shard_map(body, mesh=mesh, in_specs=in_specs, out_specs=out_specs, check_vma=False)
```

profile of v0, /device:TPU:0, one launch (start us, length us, event | category | flops | bytes accessed | tf_op | source)
XLA Modules:
  0.0 252.7 jit_solution(13355432846385626689)
XLA Ops:
  7.2 0.7 all-gather.3.cloned.1.call-update
  7.9 1.3 reduce_sum.87
  9.2 0.7 and_select_fusion
  9.9 0.7 select_reduce_fusion.2
  11.3 23.6 %all-reduce.1 = (f32[2]{0:T(128)S(1)}, f32[]{:T(128)}) all-reduce(f32[2]{0:T(128)S(1)} %select_reduce_fusion.2, f32[]{:T(128)S(6)} %convert_element_type.57), channel_id=1, replica_groups=mesh['dp'=8,'fsdp'=4] {'dp'}, use_global_device_ids=true, to_apply=%region_1.2 | all-reduce | flops 3 | bytes 24 | tf_op jit(solution)/shard_map/psum | solution.py:33
  34.9 0.7 reshape.67
  35.6 5.4 %all-gather = bf16[4,1,1280]{2,1,0:T(2,128)(2,1)S(1)} all-gather(bf16[1,1,1280]{2,1,0:T(2,128)(2,1)S(1)} %reshape.67), channel_id=1, replica_groups=mesh['dp'=8,'fsdp'=4] {'fsdp'}, dimensions={0}, use_global_device_ids=true | all-gather | bytes 12800 | tf_op jit(solution)/shard_map/all_gather | solution.py:20
  41.1 0.7 subtract_bitcast_fusion
  41.8 0.2 select_reduce_fusion.1
  41.9 0.7 multiply_subtract_fusion
  42.6 0.1 broadcast_bitcast_fusion
  42.7 0.7 copy.15
  43.4 0.7 iota_compare_fusion.1
  44.8 8.0 %all-gather.3.cloned.1.call-done = bf16[2,256,5120]{2,1,0:T(8,128)(2,1)} async-done(((bf16[2,256,1280]{2,1,0:T(8,128)(2,1)}), bf16[2,256,5120]{2,1,0:T(8,128)(2,1)}) %all-gather.3.cloned.1.call-update) | async-done | bytes 5242896 | tf_op jit(solution)/shard_map/all_gather | solution.py:19
  52.8 3.7 %multiply_reduce_fusion = f32[2,256]{1,0:T(2,128)S(1)} fusion(bf16[2,256,5120]{2,1,0:T(8,128)(2,1)} %all-gather.3.cloned.1.call-done), kind=kLoop, calls=%fused_computation.3 | loop fusion | flops 7863808 | bytes 5244928 | tf_op jit(solution)/shard_map/reduce_sum | solution.py:43
  56.6 0.3 copy-done
  56.9 2.0 fusion.1
  58.9 2.9 %fusion.15 = (f32[512]{0:T(512)S(1)}, f32[512,512]{0,1:T(8,128)S(1)}) fusion(bf16[512,5120]{1,0:T(8,128)(2,1)S(1)} %fusion.1, bf16[512,5120]{1,0:T(8,128)(2,1)S(1)} %bitcast.29), kind=kOutput, calls=%fused_computation.47 | convolution fusion | flops 2684616192 | bytes 11536384 | tf_op jit(solution)/shard_map/dot_general | solution.py:46
  61.8 5.9 %pmax.7 = f32[512]{0:T(512)S(1)} all-reduce(f32[512]{0:T(512)S(1)} %get-tuple-element.16), channel_id=1, replica_groups=mesh['dp'=8,'fsdp'=4] {'fsdp'}, use_global_device_ids=true, to_apply=%region_7.8 | all-reduce | flops 512 | bytes 4096 | tf_op jit(solution)/shard_map/pmax | solution.py:54
  67.7 0.3 exponential_reduce_fusion
  68.0 5.7 %all-reduce.2 = (f32[512]{0:T(512)S(1)}, f32[512]{0:T(512)S(1)}) all-reduce(f32[512]{0:T(512)S(1)} %get-tuple-element.7, f32[512]{0:T(512)S(1)} %exponential_multiply_fusion), channel_id=1, replica_groups=mesh['dp'=8,'fsdp'=4] {'fsdp'}, use_global_device_ids=true, to_apply=%region_5.6 | all-reduce | flops 1024 | bytes 8192 | tf_op jit(solution)/shard_map/psum | solution.py:55
  73.7 7.3 %convolution_convert_fusion.1 = bf16[512,5120]{1,0:T(8,128)(2,1)} fusion(bf16[512,5120]{1,0:T(8,128)(2,1)} %param.10, f32[512,512]{0,1:T(8,128)S(1)} %get-tuple-element.17, f32[512]{0:T(512)S(1)} %get-tuple-element.15, f32[512]{0:T(512)S(1)} %get-tuple-element.14, s32[512]{0:T(512)S(1)} %bitcast.33), kind=kOutput, calls=%fused_computation.5 | convolution fusion | flops 2688548864 | bytes 11540480 | tf_op jit(solution)/shard_map/dot_general | solution.py:69
  81.1 7.5 %convolution_convert_fusion = bf16[5120,512]{1,0:T(8,128)(2,1)} fusion(bf16[512,5120]{1,0:T(8,128)(2,1)} %copy-done.3, f32[512,512]{0,1:T(8,128)S(1)} %get-tuple-element.17, f32[512]{0:T(512)S(1)} %get-tuple-element.15, f32[512]{0:T(512)S(1)} %get-tuple-element.14, s32[512]{0:T(512)S(1)} %bitcast.34), kind=kOutput, calls=%fused_computation.4 | convolution fusion | flops 2688548864 | bytes 11540480 | tf_op jit(solution)/shard_map/dot_general | solution.py:80
  88.6 0.7 copy-done.4
  89.3 0.6 fusion.13
  89.9 43.8 %reduce-scatter.3.cloned.1.call-done = bf16[512,1280]{1,0:T(8,128)(2,1)} async-done(((bf16[512,5120]{1,0:T(8,128)(2,1)}), bf16[512,1280]{1,0:T(8,128)(2,1)}) %reduce-scatter.3.cloned.1.call-update) | async-done | bytes 1310736 | tf_op jit(solution)/shard_map/reduce_scatter | solution.py:72
  133.7 2.4 fusion.11
  136.1 23.6 %all-reduce = (f32[]{:T(128)}, f32[1280]{0:T(1024)}) all-reduce(f32[]{:T(128)} %fusion.13, f32[1280]{0:T(1024)S(1)} %get-tuple-element.4), channel_id=1, replica_groups=mesh['dp'=8,'fsdp'=4] {'dp'}, use_global_device_ids=true, to_apply=%region_11.12 | all-reduce | flops 1281 | bytes 10248 | tf_op jit(solution)/shard_map/psum | solution.py:87
  161.1 6.1 %psum.54 = f32[512]{0:T(512)S(1)} all-reduce(f32[512]{0:T(512)S(1)} %get-tuple-element.5), channel_id=1, replica_groups=mesh['dp'=8,'fsdp'=4] {'fsdp'}, use_global_device_ids=true, to_apply=%region_16.17 | all-reduce | flops 512 | bytes 4096 | tf_op jit(solution)/shard_map/psum | solution.py:75
  167.1 73.6 %reduce-scatter.5.cloned.1.call-done = bf16[640,512]{1,0:T(8,128)(2,1)} async-done(((bf16[5120,512]{1,0:T(8,128)(2,1)}), bf16[640,512]{1,0:T(8,128)(2,1)}) %reduce-scatter.5.cloned.1.call-update) | async-done | bytes 655376 | tf_op jit(solution)/shard_map/reduce_scatter | solution.py:79
  240.7 2.3 convert_element_type.67
  243.0 2.0 fusion.4
  (27 shorter events, 0.3 us)
Async XLA Ops:
  7.2 45.6 %all-gather.3.cloned.1.call-start = ((), (), s32[]{:S(2)}) async-start(), calls=%async_computation.2 | async-start | bytes 6553600 | tf_op jit(solution)/shard_map/all_gather | solution.py:19
  7.9 125.8 %reduce-scatter.3.cloned.1.call-start = ((), (), s32[]{:S(2)}) async-start(), calls=%async_computation.3 | async-start | bytes 6553600 | tf_op jit(solution)/shard_map/reduce_scatter | solution.py:72
  52.8 4.0 %copy-start = (bf16[2,256,5120]{2,1,0:T(8,128)(2,1)S(1)}, bf16[2,256,5120]{2,1,0:T(8,128)(2,1)}, u32[]{:S(2)}) copy-start(bf16[2,256,5120]{2,1,0:T(8,128)(2,1)} %all-gather.3.cloned.1.call-done) | copy-start | bytes 15728644
  52.8 6.1 %slice-start = ((s8[5242880]{0:T(1024)(128)(4,1)}), s8[4194304]{0:T(1024)(128)(4,1)S(1)}, s32[]{:S(2)}) async-start(s8[5242880]{0:T(1024)(128)(4,1)} %bitcast.28), calls=%async_computation.5 | async-start | bytes 8388608
  56.9 2.0 slice-start.1
  58.9 2.9 %copy-start.3 = (bf16[512,5120]{1,0:T(8,128)(2,1)}, bf16[512,5120]{1,0:T(8,128)(2,1)S(1)}, u32[]{:S(2)}) copy-start(bf16[512,5120]{1,0:T(8,128)(2,1)S(1)} %fusion.1) | copy-start | bytes 15728644
  81.0 159.7 %reduce-scatter.5.cloned.1.call-start = ((), (), s32[]{:S(2)}) async-start(), calls=%async_computation.4 | async-start | bytes 5898240 | tf_op jit(solution)/shard_map/reduce_scatter | solution.py:79
  88.6 0.7 copy-start.4
  88.6 45.1 %copy-start.1 = (bf16[2,256,1280]{2,1,0:T(8,128)(2,1)S(1)}, bf16[2,256,1280]{2,1,0:T(8,128)(2,1)}, u32[]{:S(2)}) copy-start(bf16[2,256,1280]{2,1,0:T(8,128)(2,1)} %param.8) | copy-start | bytes 3932164
  133.7 109.3 %copy-start.2 = (bf16[512,1280]{1,0:T(8,128)(2,1)S(1)}, bf16[512,1280]{1,0:T(8,128)(2,1)}, u32[]{:S(2)}) copy-start(bf16[512,1280]{1,0:T(8,128)(2,1)} %reduce-scatter.3.cloned.1.call-done) | copy-start | bytes 3932164
Sparse Core Ops, SparseCore 0:
  9.5 43.2 all-gather.2
  81.1 52.4 reduce-scatter.2
  137.3 103.3 reduce-scatter.4
where the time goes:
time: 253 us
  waiting for transfers between devices  126 us (50%)
  blocking collectives  70.3 us (28%)
  other arithmetic  18.4 us (7%)
  matrix products  17.7 us (7%)
  between operations  17.6 us (7%)
    reduce_scatter x1, waiting for transfers between devices, body(): lax.psum_scatter(lax.dot_general(normed, dlogits, (((0,), (0,)), ((), ())...  73.6 us
    reduce_scatter x1, waiting for transfers between devices, body(): lax.psum_scatter(dn_part.astype(jnp.bfloat16), 'fsdp', scatter_dimension=...  43.8 us
    psum x1, blocking collectives, body(): group_sums, count = lax.psum((local_sums, local_count), 'dp')  23.6 us
    psum x1, blocking collectives, body(): loss_sum, grad_gain = lax.psum((loss_local, gain_part), 'dp')  23.6 us
    all_gather x1, waiting for transfers between devices, body(): lax.all_gather(hidden, 'fsdp', axis=2, tiled=True)  8.01 us
    dot_general x1, matrix products, body(): lax.dot_general(normed, dlogits, (((0,), (0,)), ((), ())), preferred_elem...  7.54 us
    dot_general x1, matrix products, body(): dn_part = jnp.dot(dlogits, head, preferred_element_type=jnp.float32)  7.26 us
    psum x1, blocking collectives, body(): dots = lax.psum(jnp.sum(h_share * (dn_share * gain_share), axis=1), 'fsdp')  6.07 us
  transfers between devices with their start and end apart: 3, of which 3 were waited for; matrix products, arithmetic and copies ran while one was open for 7% of the time, Pallas kernels for 0%

commit v1 on v0

--- a/solution.py
+++ b/solution.py
@@ -1,6 +1,9 @@
+import functools
 import jax
 import jax.numpy as jnp
 from jax import lax
+from jax.experimental import pallas as pl
+from jax.experimental.pallas import tpu as pltpu
 from jax.sharding import PartitionSpec as P
 
 GROUP = 8
@@ -10,6 +13,253 @@
 clip_low = 0.8
 clip_high = 1.2
 dual_bound = 3.0
+
+
+MESH = pl.DeviceIdType.MESH
+
+
+def tail_kernel(
+    n_dp,
+    n_fsdp,
+    feats,
+    normed_ref,
+    dlogits_ref,
+    head_ref,
+    hidden_ref,
+    gain_ref,
+    inv_ref,
+    loss_ref,
+    gh_ref,
+    gw_ref,
+    gg_ref,
+    x_out,
+    x_in,
+    z_out,
+    z_in,
+    c_out,
+    c_in,
+    y_out,
+    y_in,
+    acc,
+    d_out,
+    d_in,
+    g_out,
+    g_in,
+    xs,
+    xr,
+    zs,
+    zr,
+    cs,
+    cr,
+    ys,
+    yr,
+    ds_,
+    dr,
+    gs,
+    gr,
+):
+    dp = lax.axis_index("dp")
+    fs = lax.axis_index("fsdp")
+    z, x = dp // 2, dp % 2
+    y, c = fs // 2, fs % 2
+    outer_dp, outer_fs = n_dp // 2, n_fsdp // 2
+    cols = hidden_ref.shape[1]
+
+    barrier = pltpu.get_barrier_semaphore()
+    for k in range(1, n_dp):
+        pl.semaphore_signal(barrier, inc=1, device_id=(dp ^ k, fs), device_id_type=MESH)
+    for k in range(1, n_fsdp):
+        pl.semaphore_signal(barrier, inc=1, device_id=(dp, fs ^ k), device_id_type=MESH)
+    pl.semaphore_wait(barrier, n_dp + n_fsdp - 2)
+
+    def remote(out, into, send, recv, k, dst):
+        return pltpu.make_async_remote_copy(
+            src_ref=out,
+            dst_ref=into.at[k],
+            send_sem=send.at[k],
+            recv_sem=recv.at[k],
+            device_id=dst,
+            device_id_type=MESH,
+        )
+
+    def x_copy(k):
+        return remote(x_out.at[k], x_in, xs, xr, k, (dp ^ 1, fs))
+
+    def z_copy(k):
+        return remote(z_out.at[k], z_in, zs, zr, k, ((z ^ k) * 2 + x, fs))
+
+    def c_copy(j):
+        return remote(c_out.at[j], c_in, cs, cr, j, (dp, fs ^ 1))
+
+    def y_copy(j):
+        return remote(y_out.at[j], y_in, ys, yr, j, (dp, (y ^ j) * 2 + c))
+
+    def d_copy(j):
+        return remote(d_out, d_in, ds_, dr, j, (dp, fs ^ j))
+
+    def g_copy(k):
+        return remote(g_out, g_in, gs, gr, k, (dp ^ k, fs))
+
+    def dw(block):
+        if feats % 128 == 0:
+            left = normed_ref[:, pl.ds(pl.multiple_of(block * feats, 128), feats)]
+        else:
+            left = normed_ref[block]
+        return lax.dot_general(
+            left, dlogits_ref[...], (((0,), (0,)), ((), ())), preferred_element_type=jnp.float32
+        )
+
+    def dn(block):
+        right = head_ref[:, pl.ds(pl.multiple_of(block * cols, 128), cols)]
+        return jnp.dot(dlogits_ref[...], right, preferred_element_type=jnp.float32)
+
+    @pl.loop(0, outer_dp)
+    def _(i):
+        k = outer_dp - 1 - i
+        x_out[k] = dw((z ^ k) * 2 + (1 - x)).astype(jnp.bfloat16)
+        x_copy(k).start()
+
+    @pl.loop(0, outer_fs)
+    def _(i):
+        j = outer_fs - 1 - i
+        c_out[j] = dn((y ^ j) * 2 + (1 - c)).astype(jnp.bfloat16)
+        c_copy(j).start()
+
+    @pl.loop(0, outer_fs - 1)
+    def _(i):
+        j = outer_fs - 1 - i
+        mine = dn((y ^ j) * 2 + c)
+        c_copy(j).wait_recv()
+        y_out[j] = (mine + c_in[j].astype(jnp.float32)).astype(jnp.bfloat16)
+        y_copy(j).start()
+
+    acc[...] = dn(fs)
+    c_copy(0).wait_recv()
+    acc[...] += c_in[0].astype(jnp.float32)
+
+    @pl.loop(0, outer_dp - 1)
+    def _(i):
+        k = outer_dp - 1 - i
+        mine = dw((z ^ k) * 2 + x)
+        x_copy(k).wait_recv()
+        z_out[k] = (mine + x_in[k].astype(jnp.float32)).astype(jnp.bfloat16)
+        z_copy(k).start()
+
+    @pl.loop(1, outer_fs)
+    def _(j):
+        y_copy(j).wait_recv()
+        acc[...] += y_in[j].astype(jnp.float32)
+
+    h = hidden_ref[...].astype(jnp.float32)
+    inv = inv_ref[...]
+    g_out[:, :cols] = jnp.broadcast_to(
+        jnp.sum(acc[...] * h * inv, axis=0, keepdims=True), (8, cols)
+    )
+    g_out[:, cols:] = loss_ref[...]
+
+    @pl.loop(1, n_dp)
+    def _(k):
+        g_copy(k).start()
+
+    dy = acc[...] * gain_ref[...]
+    part = jnp.sum(h * dy, axis=1, keepdims=True)
+    rows = part.shape[0]
+    d_out[...] = jnp.transpose(jnp.broadcast_to(part, (rows, 128)))[:8]
+    for j in range(1, n_fsdp):
+        d_copy(j).start()
+    dots = d_out[...]
+    for j in range(1, n_fsdp):
+        d_copy(j).wait_recv()
+        dots += d_in[j]
+    column = jnp.transpose(jnp.broadcast_to(dots[:1], (128, rows)))[:, :1]
+    scale = inv * inv * inv * column / (cols * n_fsdp)
+    gh_ref[...] = (
+        inv * (acc[...] * gain_ref[...]) - hidden_ref[...].astype(jnp.float32) * scale
+    ).astype(jnp.bfloat16)
+
+    gg_ref[...] = g_out[...]
+
+    @pl.loop(1, n_dp)
+    def _(k):
+        g_copy(k).wait_recv()
+        gg_ref[...] += g_in[k]
+
+    own = dw(dp)
+    x_copy(0).wait_recv()
+    gw_ref[...] = own + x_in[0].astype(jnp.float32)
+
+    @pl.loop(0, outer_dp - 1)
+    def _(i):
+        k = outer_dp - 1 - i
+        z_copy(k).wait_recv()
+        gw_ref[...] += z_in[k].astype(jnp.float32)
+
+    @pl.loop(0, outer_dp)
+    def _(k):
+        x_copy(k).wait_send()
+
+    @pl.loop(1, outer_dp)
+    def _(k):
+        z_copy(k).wait_send()
+
+    @pl.loop(0, outer_fs)
+    def _(j):
+        c_copy(j).wait_send()
+
+    @pl.loop(1, outer_fs)
+    def _(j):
+        y_copy(j).wait_send()
+
+    for j in range(1, n_fsdp):
+        d_copy(j).wait_send()
+
+    @pl.loop(1, n_dp)
+    def _(k):
+        g_copy(k).wait_send()
+
+
+def tail(normed, dlogits, head, hidden, gain_row, inv, loss_tile):
+    n_dp, n_fsdp = lax.axis_size("dp"), lax.axis_size("fsdp")
+    rows, width = normed.shape
+    vocab_here = head.shape[0]
+    cols = hidden.shape[1]
+    feats = width // n_dp
+    zd, yd = n_dp // 2, n_fsdp // 2
+    if feats % 128:
+        normed = normed.reshape(rows, n_dp, feats).transpose(1, 0, 2)
+    wide = cols + 128
+    bf, f32 = jnp.bfloat16, jnp.float32
+    vm = pl.BlockSpec(memory_space=pltpu.VMEM)
+    dma = pltpu.SemaphoreType.DMA
+    return pl.pallas_call(
+        functools.partial(tail_kernel, n_dp, n_fsdp, feats),
+        out_shape=(
+            jax.ShapeDtypeStruct((rows, cols), bf),
+            jax.ShapeDtypeStruct((feats, vocab_here), f32),
+            jax.ShapeDtypeStruct((8, wide), f32),
+        ),
+        in_specs=[vm] * 7,
+        out_specs=(vm, vm, vm),
+        scratch_shapes=[
+            pltpu.VMEM((zd, feats, vocab_here), bf),
+            pltpu.VMEM((zd, feats, vocab_here), bf),
+            pltpu.VMEM((zd, feats, vocab_here), bf),
+            pltpu.VMEM((zd, feats, vocab_here), bf),
+            pltpu.VMEM((yd, rows, cols), bf),
+            pltpu.VMEM((yd, rows, cols), bf),
+            pltpu.VMEM((yd, rows, cols), bf),
+            pltpu.VMEM((yd, rows, cols), bf),
+            pltpu.VMEM((rows, cols), f32),
+            pltpu.VMEM((8, rows), f32),
+            pltpu.VMEM((n_fsdp, 8, rows), f32),
+            pltpu.VMEM((8, wide), f32),
+            pltpu.VMEM((n_dp, 8, wide), f32),
+        ]
+        + [dma((n,)) for n in (zd, zd, zd, zd, yd, yd, yd, yd, n_fsdp, n_fsdp, n_dp, n_dp)],
+        compiler_params=pltpu.CompilerParams(
+            collective_id=0, has_side_effects=True, vmem_limit_bytes=60 * 1024 * 1024
+        ),
+    )(normed, dlogits, head, hidden, gain_row, inv, loss_tile)
 
 
 def body(hidden, gain, head, targets, lengths, old_logp, rewards, group_slot):
@@ -51,8 +301,10 @@
     local_targets = targets.reshape(rows) - vocab_start
     hits = jnp.arange(vocab_here, dtype=jnp.int32)[None, :] == local_targets[:, None]
     chosen_local = jnp.sum(jnp.where(hits, logits, 0.0), axis=1)
-    top = lax.pmax(top_local, "fsdp")
-    total, chosen = lax.psum((sum_local * jnp.exp(top_local - top), chosen_local), "fsdp")
+    stats = lax.all_gather(jnp.stack([top_local, sum_local, chosen_local]), "fsdp", axis=0)
+    top = jnp.max(stats[:, 0], axis=0)
+    total = jnp.sum(stats[:, 1] * jnp.exp(stats[:, 0] - top[None, :]), axis=0)
+    chosen = jnp.sum(stats[:, 2], axis=0)
     lse = top + jnp.log(total)
     logp = chosen - lse
     ratio = jnp.exp(logp - old_logp.reshape(rows))
@@ -66,27 +318,18 @@
     grad_logp = slots_all / count * mask * jnp.where(active, -ratio * adv, 0.0)
     probs = jnp.exp(logits - lse[:, None])
     dlogits = (grad_logp[:, None] * (hits.astype(jnp.float32) - probs)).astype(jnp.bfloat16)
-    dn_part = jnp.dot(dlogits, head, preferred_element_type=jnp.float32)
-    h_share = hidden.reshape(rows, shard_cols).astype(jnp.float32)
-    gain_share = gain.astype(jnp.float32)
-    dn_share = lax.psum_scatter(
-        dn_part.astype(jnp.bfloat16), "fsdp", scatter_dimension=1, tiled=True
-    ).astype(jnp.float32)
-    dots = lax.psum(jnp.sum(h_share * (dn_share * gain_share), axis=1), "fsdp")
-    dy = dn_share * gain_share
-    grad_h = inv * dy - h_share * inv * inv * inv * dots[:, None] / width
-    gain_part = jnp.sum(dn_share * h_share * inv, axis=0)
-    grad_head_t = lax.psum_scatter(
-        lax.dot_general(
-            normed, dlogits, (((0,), (0,)), ((), ())), preferred_element_type=jnp.float32
-        ).astype(jnp.bfloat16),
-        "dp",
-        scatter_dimension=0,
-        tiled=True,
-    ).astype(jnp.float32)
-    loss_sum, grad_gain = lax.psum((loss_local, gain_part), "dp")
-    loss = loss_sum / count
-    grad_hidden = grad_h.astype(jnp.bfloat16).reshape(resp_here, length_max, shard_cols)
+    grad_h, grad_head_t, sums = tail(
+        normed,
+        dlogits,
+        head,
+        hidden.reshape(rows, shard_cols),
+        gain.astype(jnp.float32)[None, :],
+        inv,
+        jnp.broadcast_to(loss_local, (8, 128)),
+    )
+    loss = sums[0, shard_cols] / count
+    grad_gain = sums[0, :shard_cols]
+    grad_hidden = grad_h.reshape(resp_here, length_max, shard_cols)
     return (loss, grad_hidden, grad_gain, grad_head_t)
 
 

time: 253 us -> 182 us (0.72)
  waiting for transfers between devices: 126 us -> 7.47 us
  Pallas kernels: 0 us -> 92.4 us
  blocking collectives: 70.3 us -> 34.4 us
  matrix products: 17.7 us -> 2.91 us
  local copies, waits for them, and re-layouts: 2.44 us -> 13 us
  other arithmetic: 18.4 us -> 13.1 us
    reduce_scatter x2 -> x0, waiting for transfers between devices: 117 us -> none  [the longest x1 73.6 us: body(): lax.psum_scatter(lax.dot_general(normed, dlogits, (((0,), (0,)), ((), ())...]
    pallas_call x0 -> x1, Pallas kernels: none -> 92.4 us  [tail(): pl.pallas_call(functools.partial(tail_kernel, n_dp, n_fsdp, feats), out_s...]
    psum x3 -> x0, blocking collectives: 35.4 us -> none  [the longest x1 23.6 us: body(): loss_sum, grad_gain = lax.psum((loss_local, gain_part), 'dp')]
    dot_general x2 -> x0, matrix products: 14.8 us -> none  [the longest x1 7.54 us: body(): lax.dot_general(normed, dlogits, (((0,), (0,)), ((), ())), preferred_elem...]
    pmax x1 -> x0, blocking collectives: 5.9 us -> none  [body(): top = lax.pmax(top_local, 'fsdp')]
    all_gather x0 -> x1, blocking collectives: none -> 5.37 us  [body(): lax.all_gather(jnp.stack([top_local, sum_local, chosen_local]), 'fsdp', a...]
    unnamed x20 -> x23, local copies, waits for them, and re-layouts: 2.42 us -> 7.56 us
    convert_element_type x3 -> x1, other arithmetic: 4.31 us -> 1.13 us  [body(): (grad_logp[:, None] * (hits.astype(jnp.float32) - probs)).astype(jnp.bflo...]
  transfers between devices with their start and end apart: 3 -> 1, of which waited for: 3 -> 1; matrix products, arithmetic and copies ran while one was open for 7% -> 4% of each run, Pallas kernels for 0% -> 0%
where the time goes in v1:
time: 182 us; the launch traced here: 181 us
  Pallas kernels  92.4 us (51%)
  blocking collectives  34.4 us (19%)
  between operations  18 us (10%)
  other arithmetic  13.1 us (7%)
  local copies, waits for them, and re-layouts  13 us (7%)
  waiting for transfers between devices  7.47 us (4%)
  matrix products  2.91 us (2%)
    pallas_call x1, Pallas kernels, tail(): pl.pallas_call(functools.partial(tail_kernel, n_dp, n_fsdp, feats), out_s...  92.4 us
    psum x1, blocking collectives, body(): group_sums, count = lax.psum((local_sums, local_count), 'dp')  23.6 us
    unnamed x23, local copies, waits for them, and re-layouts  7.56 us
    all_gather x1, waiting for transfers between devices, body(): lax.all_gather(hidden, 'fsdp', axis=2, tiled=True)  6.79 us
    all_gather x1, blocking collectives, body(): lax.all_gather(gain, 'fsdp', axis=0, tiled=True)  5.42 us
    all_gather x1, blocking collectives, body(): lax.all_gather(jnp.stack([top_local, sum_local, chosen_local]), 'fsdp', a...  5.37 us
    reduce_sum x1, other arithmetic, body(): jnp.mean(jnp.square(whole.astype(jnp.float32)), axis=1, keepdims=True)  3.74 us
  transfers between devices with their start and end apart: 1, of which 1 were waited for; matrix products, arithmetic and copies ran while one was open for 4% of the time, Pallas kernels for 0%

profile of v1, /device:TPU:0, one launch (start us, length us, event | category | flops | bytes accessed | tf_op | source)
XLA Modules:
  0.0 181.3 jit_solution(871954883184080322)
XLA Ops:
  7.2 0.7 all-gather.5.cloned.1.call-update
  7.9 1.3 reduce_sum.82
  9.2 0.7 and_select_fusion
  9.9 0.7 select_reduce_fusion.2
  11.2 23.6 %all-reduce = (f32[]{:T(128)}, f32[2]{0:T(128)S(1)}) all-reduce(f32[]{:T(128)S(6)} %convert_element_type.36, f32[2]{0:T(128)S(1)} %select_reduce_fusion.2), channel_id=1, replica_groups=mesh['dp'=8,'fsdp'=4] {'dp'}, use_global_device_ids=true, to_apply=%region_2.3 | all-reduce | flops 3 | bytes 24 | tf_op jit(solution)/shard_map/psum | solution.py:283
  34.9 0.7 reshape.149
  35.6 1.3 reshape.147.gain_ref
  36.9 5.4 %all-gather.1 = bf16[4,1,1280]{2,1,0:T(2,128)(2,1)S(1)} all-gather(bf16[1,1,1280]{2,1,0:T(2,128)(2,1)S(1)} %reshape.149), channel_id=1, replica_groups=mesh['dp'=8,'fsdp'=4] {'fsdp'}, dimensions={0}, use_global_device_ids=true | all-gather | bytes 12800 | tf_op jit(solution)/shard_map/all_gather | solution.py:270
  42.3 0.7 subtract_bitcast_fusion
  43.0 0.2 select_reduce_fusion.1
  43.2 0.7 broadcast_multiply_fusion
  43.8 0.1 broadcast_bitcast_fusion
  44.6 0.7 select_bitcast_fusion
  45.3 0.7 copy.32
  46.0 6.8 %all-gather.5.cloned.1.call-done = bf16[2,256,5120]{2,1,0:T(8,128)(2,1)} async-done(((bf16[2,256,1280]{2,1,0:T(8,128)(2,1)}), bf16[2,256,5120]{2,1,0:T(8,128)(2,1)}) %all-gather.5.cloned.1.call-update) | async-done | bytes 5242896 | tf_op jit(solution)/shard_map/all_gather | solution.py:269
  52.8 3.7 %multiply_reduce_fusion = f32[2,256]{1,0:T(2,128)S(1)} fusion(bf16[2,256,5120]{2,1,0:T(8,128)(2,1)} %all-gather.5.cloned.1.call-done), kind=kLoop, calls=%fused_computation.3 | loop fusion | flops 7863808 | bytes 5244928 | tf_op jit(solution)/shard_map/reduce_sum | solution.py:293
  56.6 0.3 copy-done
  56.9 2.0 %fusion.1.normed_ref = bf16[512,5120]{1,0:T(8,128)(2,1)S(1)} fusion(f32[5120]{0:T(1024)S(1)} %bitcast.53, f32[512]{0:T(512)S(1)} %bitcast.64, bf16[2,256,5120]{2,1,0:T(8,128)(2,1)S(1)} %copy-done), kind=kLoop, calls=%fused_computation.2 | loop fusion | flops 10485760 | bytes 10508288 | tf_op jit(solution)/shard_map/convert_element_type | solution.py:295
  58.9 2.9 %fusion.11 = (f32[512]{0:T(512)S(1)}, f32[512,512]{0,1:T(8,128)S(1)}) fusion(bf16[512,5120]{1,0:T(8,128)(2,1)S(1)} %fusion.1.normed_ref, bf16[512,5120]{1,0:T(8,128)(2,1)S(1)} %bitcast.49), kind=kOutput, calls=%fused_computation.44 | convolution fusion | flops 2684616192 | bytes 11536384 | tf_op jit(solution)/shard_map/dot_general | solution.py:296
  61.9 0.3 copy.23
  62.2 0.2 exponential_reduce_fusion
  62.4 0.3 select_reduce_fusion
  62.7 5.4 %all-gather.2 = f32[4,3,512]{2,1,0:T(4,128)S(1)} all-gather(f32[1,3,512]{2,1,0:T(4,128)S(1)} %maximum_bitcast_fusion), channel_id=2, replica_groups=mesh['dp'=8,'fsdp'=4] {'fsdp'}, dimensions={0}, use_global_device_ids=true | all-gather | bytes 30720 | tf_op jit(solution)/shard_map/all_gather | solution.py:304
  68.2 0.9 copy.35
  69.0 1.1 multiply_convert_fusion.dlogits_ref
  70.2 0.7 fusion.8
  70.9 1.2 broadcast_in_dim.41.loss_ref
  72.1 92.4 %shard_map.111 = (bf16[512,1280]{1,0:T(8,128)(2,1)}, f32[640,512]{1,0:T(8,128)}, f32[8,1408]{1,0:T(8,128)}) custom-call(bf16[512,5120]{1,0:T(8,128)(2,1)} %copy-done.1, bf16[512,512]{1,0:T(8,128)(2,1)} %multiply_convert_fusion.dlogits_ref, bf16[512,5120]{1,0:T(8,128)(2,1)} %head_ref.1, bf16[512,1280]{1,0:T(8,128)(2,1)} %bitcast.50, ...), custom_call_target="tpu_custom_call" | custom-call | tf_op jit(solution)/shard_map/pallas_call | solution.py:234
  164.5 1.4 slice_reduce_fusion.1
  165.9 1.2 slice.19
  168.4 2.5 %copy.44 = bf16[2,256,1280]{2,1,0:T(8,128)(2,1)} copy(bf16[2,256,1280]{2,1,0:T(8,128)(2,1)} %bitcast.51) | data formatting | bytes 2621440
  170.9 2.5 %copy.45 = f32[640,512]{1,0:T(8,128)} copy(f32[640,512]{1,0:T(8,128)} %get-tuple-element.32) | data formatting | bytes 2621440
  (26 shorter events, 0.2 us)
Async XLA Ops:
  7.2 45.6 %all-gather.5.cloned.1.call-start = ((), (), s32[]{:S(2)}) async-start(), calls=%async_computation | async-start | bytes 6553600 | tf_op jit(solution)/shard_map/all_gather | solution.py:269
  52.8 4.0 %copy-start = (bf16[2,256,5120]{2,1,0:T(8,128)(2,1)S(1)}, bf16[2,256,5120]{2,1,0:T(8,128)(2,1)}, u32[]{:S(2)}) copy-start(bf16[2,256,5120]{2,1,0:T(8,128)(2,1)} %all-gather.5.cloned.1.call-done) | copy-start | bytes 15728644
  52.8 6.1 %slice-start = ((s8[5242880]{0:T(1024)(128)(4,1)}), s8[4194304]{0:T(1024)(128)(4,1)S(1)}, s32[]{:S(2)}) async-start(s8[5242880]{0:T(1024)(128)(4,1)} %bitcast.48), calls=%async_computation.1 | async-start | bytes 8388608
  56.9 2.0 %slice-start.1 = ((s8[5242880]{0:T(1024)(128)(4,1)}), s8[1048576]{0:T(1024)(128)(4,1)S(1)}, s32[]{:S(2)}) async-start(s8[5242880]{0:T(1024)(128)(4,1)} %bitcast.48), calls=%async_computation.2 | async-start | bytes 2097152
  58.9 2.9 %copy-start.1 = (bf16[512,5120]{1,0:T(8,128)(2,1)}, bf16[512,5120]{1,0:T(8,128)(2,1)S(1)}, u32[]{:S(2)}) copy-start(bf16[512,5120]{1,0:T(8,128)(2,1)S(1)} %fusion.1.normed_ref) | copy-start | bytes 15728644
  61.8 8.3 %copy-start.2 = (f32[2,256]{1,0:T(2,128)S(1)}, f32[2,256]{1,0:T(2,128)}, u32[]{:S(2)}) copy-start(f32[2,256]{1,0:T(2,128)} %param.13) | copy-start | bytes 6148
  61.9 8.3 %copy-start.3 = (s32[2]{0:T(128)S(1)}, s32[2]{0:T(128)}, u32[]{:S(2)}) copy-start(s32[2]{0:T(128)} %param.12) | copy-start | bytes 28
Sparse Core Ops, SparseCore 0:
  9.5 43.2 all-gather.4

commit v2 on v1

--- a/solution.py
+++ b/solution.py
@@ -34,6 +34,8 @@
     gg_ref,
     x_out,
     x_in,
+    n_out,
+    n_in,
     z_out,
     z_in,
     c_out,
@@ -47,6 +49,8 @@
     g_in,
     xs,
     xr,
+    ns,
+    nr,
     zs,
     zr,
     cs,
@@ -62,7 +66,7 @@
     fs = lax.axis_index("fsdp")
     z, x = dp // 2, dp % 2
     y, c = fs // 2, fs % 2
-    outer_dp, outer_fs = n_dp // 2, n_fsdp // 2
+    outer_dp, outer_fs, quads = n_dp // 2, n_fsdp // 2, n_dp // 4
     cols = hidden_ref.shape[1]
 
     barrier = pltpu.get_barrier_semaphore()
@@ -86,7 +90,10 @@
         return remote(x_out.at[k], x_in, xs, xr, k, (dp ^ 1, fs))
 
     def z_copy(k):
-        return remote(z_out.at[k], z_in, zs, zr, k, ((z ^ k) * 2 + x, fs))
+        return remote(z_out.at[k], z_in, zs, zr, k, (dp ^ (4 * k), fs))
+
+    def n_copy(k):
+        return remote(n_out.at[k], n_in, ns, nr, k, (dp ^ 2, fs))
 
     def c_copy(j):
         return remote(c_out.at[j], c_in, cs, cr, j, (dp, fs ^ 1))
@@ -137,13 +144,25 @@
     c_copy(0).wait_recv()
     acc[...] += c_in[0].astype(jnp.float32)
 
-    @pl.loop(0, outer_dp - 1)
-    def _(i):
-        k = outer_dp - 1 - i
+    def pair_sum(k):
         mine = dw((z ^ k) * 2 + x)
         x_copy(k).wait_recv()
-        z_out[k] = (mine + x_in[k].astype(jnp.float32)).astype(jnp.bfloat16)
-        z_copy(k).start()
+        return mine + x_in[k].astype(jnp.float32)
+
+    def to_near(q):
+        n_out[q] = pair_sum(2 * q + 1).astype(jnp.bfloat16)
+        n_copy(q).start()
+
+    @pl.loop(0, quads - 1)
+    def _(i):
+        q = quads - 1 - i
+        to_near(q)
+        mine = pair_sum(2 * q)
+        n_copy(q).wait_recv()
+        z_out[q] = (mine + n_in[q].astype(jnp.float32)).astype(jnp.bfloat16)
+        z_copy(q).start()
+
+    to_near(0)
 
     @pl.loop(1, outer_fs)
     def _(j):
@@ -184,13 +203,12 @@
         g_copy(k).wait_recv()
         gg_ref[...] += g_in[k]
 
-    own = dw(dp)
-    x_copy(0).wait_recv()
-    gw_ref[...] = own + x_in[0].astype(jnp.float32)
-
-    @pl.loop(0, outer_dp - 1)
-    def _(i):
-        k = outer_dp - 1 - i
+    gw_ref[...] = pair_sum(0)
+    n_copy(0).wait_recv()
+    gw_ref[...] += n_in[0].astype(jnp.float32)
+
+    @pl.loop(1, quads)
+    def _(k):
         z_copy(k).wait_recv()
         gw_ref[...] += z_in[k].astype(jnp.float32)
 
@@ -198,7 +216,11 @@
     def _(k):
         x_copy(k).wait_send()
 
-    @pl.loop(1, outer_dp)
+    @pl.loop(0, quads)
+    def _(k):
+        n_copy(k).wait_send()
+
+    @pl.loop(1, quads)
     def _(k):
         z_copy(k).wait_send()
 
@@ -224,7 +246,7 @@
     vocab_here = head.shape[0]
     cols = hidden.shape[1]
     feats = width // n_dp
-    zd, yd = n_dp // 2, n_fsdp // 2
+    zd, qd, yd = n_dp // 2, n_dp // 4, n_fsdp // 2
     if feats % 128:
         normed = normed.reshape(rows, n_dp, feats).transpose(1, 0, 2)
     wide = cols + 128
@@ -243,8 +265,10 @@
         scratch_shapes=[
             pltpu.VMEM((zd, feats, vocab_here), bf),
             pltpu.VMEM((zd, feats, vocab_here), bf),
-            pltpu.VMEM((zd, feats, vocab_here), bf),
-            pltpu.VMEM((zd, feats, vocab_here), bf),
+            pltpu.VMEM((qd, feats, vocab_here), bf),
+            pltpu.VMEM((qd, feats, vocab_here), bf),
+            pltpu.VMEM((qd, feats, vocab_here), bf),
+            pltpu.VMEM((qd, feats, vocab_here), bf),
             pltpu.VMEM((yd, rows, cols), bf),
             pltpu.VMEM((yd, rows, cols), bf),
             pltpu.VMEM((yd, rows, cols), bf),
@@ -255,7 +279,7 @@
             pltpu.VMEM((8, wide), f32),
             pltpu.VMEM((n_dp, 8, wide), f32),
         ]
-        + [dma((n,)) for n in (zd, zd, zd, zd, yd, yd, yd, yd, n_fsdp, n_fsdp, n_dp, n_dp)],
+        + [dma((n,)) for n in (zd, zd, qd, qd, qd, qd, yd, yd, yd, yd, n_fsdp, n_fsdp, n_dp, n_dp)],
         compiler_params=pltpu.CompilerParams(
             collective_id=0, has_side_effects=True, vmem_limit_bytes=60 * 1024 * 1024
         ),

time: 182 us -> 181 us (level)
  no operation moved by 1% of the time
where the time goes in v2:
time: 181 us; the launch traced here: 180 us
  Pallas kernels  91.5 us (51%)
  blocking collectives  34.4 us (19%)
  between operations  18 us (10%)
  other arithmetic  13.1 us (7%)
  local copies, waits for them, and re-layouts  13 us (7%)
  waiting for transfers between devices  7.47 us (4%)
  matrix products  2.91 us (2%)
    pallas_call x1, Pallas kernels, tail(): pl.pallas_call(functools.partial(tail_kernel, n_dp, n_fsdp, feats), out_s...  91.5 us
    psum x1, blocking collectives, body(): group_sums, count = lax.psum((local_sums, local_count), 'dp')  23.6 us
    unnamed x23, local copies, waits for them, and re-layouts  7.56 us
    all_gather x1, waiting for transfers between devices, body(): lax.all_gather(hidden, 'fsdp', axis=2, tiled=True)  6.79 us
    all_gather x1, blocking collectives, body(): lax.all_gather(gain, 'fsdp', axis=0, tiled=True)  5.42 us
    all_gather x1, blocking collectives, body(): lax.all_gather(jnp.stack([top_local, sum_local, chosen_local]), 'fsdp', a...  5.37 us
    reduce_sum x1, other arithmetic, body(): jnp.mean(jnp.square(whole.astype(jnp.float32)), axis=1, keepdims=True)  3.74 us
  transfers between devices with their start and end apart: 1, of which 1 were waited for; matrix products, arithmetic and copies ran while one was open for 4% of the time, Pallas kernels for 0%

profile of v2, /device:TPU:0, one launch (start us, length us, event | category | flops | bytes accessed | tf_op | source)
XLA Modules:
  0.0 180.4 jit_solution(10985499645446271927)
XLA Ops:
  7.2 0.7 all-gather.5.cloned.1.call-update
  7.9 1.3 reduce_sum.82
  9.2 0.7 and_select_fusion
  9.9 0.7 select_reduce_fusion.2
  11.2 23.6 %all-reduce = (f32[]{:T(128)}, f32[2]{0:T(128)S(1)}) all-reduce(f32[]{:T(128)S(6)} %convert_element_type.36, f32[2]{0:T(128)S(1)} %select_reduce_fusion.2), channel_id=1, replica_groups=mesh['dp'=8,'fsdp'=4] {'dp'}, use_global_device_ids=true, to_apply=%region_2.3 | all-reduce | flops 3 | bytes 24 | tf_op jit(solution)/shard_map/psum | solution.py:307
  34.9 0.7 reshape.149
  35.6 1.3 reshape.147.gain_ref
  36.9 5.4 %all-gather.1 = bf16[4,1,1280]{2,1,0:T(2,128)(2,1)S(1)} all-gather(bf16[1,1,1280]{2,1,0:T(2,128)(2,1)S(1)} %reshape.149), channel_id=1, replica_groups=mesh['dp'=8,'fsdp'=4] {'fsdp'}, dimensions={0}, use_global_device_ids=true | all-gather | bytes 12800 | tf_op jit(solution)/shard_map/all_gather | solution.py:294
  42.3 0.7 subtract_bitcast_fusion
  43.0 0.2 select_reduce_fusion.1
  43.2 0.7 broadcast_multiply_fusion
  43.8 0.1 broadcast_bitcast_fusion
  44.6 0.7 select_bitcast_fusion
  45.3 0.7 copy.32
  46.0 6.8 %all-gather.5.cloned.1.call-done = bf16[2,256,5120]{2,1,0:T(8,128)(2,1)} async-done(((bf16[2,256,1280]{2,1,0:T(8,128)(2,1)}), bf16[2,256,5120]{2,1,0:T(8,128)(2,1)}) %all-gather.5.cloned.1.call-update) | async-done | bytes 5242896 | tf_op jit(solution)/shard_map/all_gather | solution.py:293
  52.8 3.7 %multiply_reduce_fusion = f32[2,256]{1,0:T(2,128)S(1)} fusion(bf16[2,256,5120]{2,1,0:T(8,128)(2,1)} %all-gather.5.cloned.1.call-done), kind=kLoop, calls=%fused_computation.3 | loop fusion | flops 7863808 | bytes 5244928 | tf_op jit(solution)/shard_map/reduce_sum | solution.py:317
  56.6 0.3 copy-done
  56.9 2.0 %fusion.1.normed_ref = bf16[512,5120]{1,0:T(8,128)(2,1)S(1)} fusion(f32[5120]{0:T(1024)S(1)} %bitcast.53, f32[512]{0:T(512)S(1)} %bitcast.64, bf16[2,256,5120]{2,1,0:T(8,128)(2,1)S(1)} %copy-done), kind=kLoop, calls=%fused_computation.2 | loop fusion | flops 10485760 | bytes 10508288 | tf_op jit(solution)/shard_map/convert_element_type | solution.py:319
  58.9 2.9 %fusion.11 = (f32[512]{0:T(512)S(1)}, f32[512,512]{0,1:T(8,128)S(1)}) fusion(bf16[512,5120]{1,0:T(8,128)(2,1)S(1)} %fusion.1.normed_ref, bf16[512,5120]{1,0:T(8,128)(2,1)S(1)} %bitcast.49), kind=kOutput, calls=%fused_computation.44 | convolution fusion | flops 2684616192 | bytes 11536384 | tf_op jit(solution)/shard_map/dot_general | solution.py:320
  61.9 0.3 copy.23
  62.2 0.2 exponential_reduce_fusion
  62.4 0.3 select_reduce_fusion
  62.7 5.4 %all-gather.2 = f32[4,3,512]{2,1,0:T(4,128)S(1)} all-gather(f32[1,3,512]{2,1,0:T(4,128)S(1)} %maximum_bitcast_fusion), channel_id=2, replica_groups=mesh['dp'=8,'fsdp'=4] {'fsdp'}, dimensions={0}, use_global_device_ids=true | all-gather | bytes 30720 | tf_op jit(solution)/shard_map/all_gather | solution.py:328
  68.2 0.9 copy.35
  69.0 1.1 multiply_convert_fusion.dlogits_ref
  70.2 0.7 fusion.8
  70.9 1.2 broadcast_in_dim.41.loss_ref
  72.1 91.5 %shard_map.111 = (bf16[512,1280]{1,0:T(8,128)(2,1)}, f32[640,512]{1,0:T(8,128)}, f32[8,1408]{1,0:T(8,128)}) custom-call(bf16[512,5120]{1,0:T(8,128)(2,1)} %copy-done.1, bf16[512,512]{1,0:T(8,128)(2,1)} %multiply_convert_fusion.dlogits_ref, bf16[512,5120]{1,0:T(8,128)(2,1)} %head_ref.1, bf16[512,1280]{1,0:T(8,128)(2,1)} %bitcast.50, ...), custom_call_target="tpu_custom_call" | custom-call | tf_op jit(solution)/shard_map/pallas_call | solution.py:256
  163.6 1.4 slice_reduce_fusion.1
  165.0 1.2 slice.19
  167.5 2.5 %copy.44 = bf16[2,256,1280]{2,1,0:T(8,128)(2,1)} copy(bf16[2,256,1280]{2,1,0:T(8,128)(2,1)} %bitcast.51) | data formatting | bytes 2621440
  170.0 2.5 %copy.45 = f32[640,512]{1,0:T(8,128)} copy(f32[640,512]{1,0:T(8,128)} %get-tuple-element.32) | data formatting | bytes 2621440
  (26 shorter events, 0.2 us)
Async XLA Ops:
  7.2 45.6 %all-gather.5.cloned.1.call-start = ((), (), s32[]{:S(2)}) async-start(), calls=%async_computation | async-start | bytes 6553600 | tf_op jit(solution)/shard_map/all_gather | solution.py:293
  52.8 4.0 %copy-start = (bf16[2,256,5120]{2,1,0:T(8,128)(2,1)S(1)}, bf16[2,256,5120]{2,1,0:T(8,128)(2,1)}, u32[]{:S(2)}) copy-start(bf16[2,256,5120]{2,1,0:T(8,128)(2,1)} %all-gather.5.cloned.1.call-done) | copy-start | bytes 15728644
  52.8 6.1 %slice-start = ((s8[5242880]{0:T(1024)(128)(4,1)}), s8[4194304]{0:T(1024)(128)(4,1)S(1)}, s32[]{:S(2)}) async-start(s8[5242880]{0:T(1024)(128)(4,1)} %bitcast.48), calls=%async_computation.1 | async-start | bytes 8388608
  56.9 2.0 %slice-start.1 = ((s8[5242880]{0:T(1024)(128)(4,1)}), s8[1048576]{0:T(1024)(128)(4,1)S(1)}, s32[]{:S(2)}) async-start(s8[5242880]{0:T(1024)(128)(4,1)} %bitcast.48), calls=%async_computation.2 | async-start | bytes 2097152
  58.9 2.9 %copy-start.1 = (bf16[512,5120]{1,0:T(8,128)(2,1)}, bf16[512,5120]{1,0:T(8,128)(2,1)S(1)}, u32[]{:S(2)}) copy-start(bf16[512,5120]{1,0:T(8,128)(2,1)S(1)} %fusion.1.normed_ref) | copy-start | bytes 15728644
  61.8 8.3 %copy-start.2 = (f32[2,256]{1,0:T(2,128)S(1)}, f32[2,256]{1,0:T(2,128)}, u32[]{:S(2)}) copy-start(f32[2,256]{1,0:T(2,128)} %param.13) | copy-start | bytes 6148
  61.9 8.3 %copy-start.3 = (s32[2]{0:T(128)S(1)}, s32[2]{0:T(128)}, u32[]{:S(2)}) copy-start(s32[2]{0:T(128)} %param.12) | copy-start | bytes 28
Sparse Core Ops, SparseCore 0:
  9.5 43.2 all-gather.4
